TPU v7x, 8 devices: a whole 2x2x1 slice. The times are simulated.
8 devices in a mesh: dp: 2 (over z, y), tp: 4 (over x, core).
Axes of the slice: x: 2, y: 2, z: 1, core: 2. Of those that a mesh axis runs over, the one named last changes fastest.
Arguments:
- x_in: bfloat16 [2, 128, 5120], P('dp', 'tp'), parts along dimension 0
- ln1_gain: float32 [2, 5120], replicated
- w_qkv: bfloat16 [2, 5120, 40, 384], P(None, None, 'tp')
- w_out: bfloat16 [2, 40, 128, 5120], P(None, 'tp')
- ln2_gain: float32 [2, 5120], replicated
- w_up: bfloat16 [2, 5120, 20480], P(None, None, 'tp')
- w_down: bfloat16 [2, 20480, 5120], P(None, 'tp')
Outputs:
- output: bfloat16 [2, 128, 5120], P('dp', 'tp'), parts along dimension 0
There are 2 independent parts. A program takes and returns all parts, laid end to end along the dimension named above; an argument that names none is the same for every part.
All inputs are finite; a program needn't handle non-finite values.
Results may differ from a plain program's by a relative error of at most 0.02.
Values are sent between devices in bfloat16 or wider.
A program may use at most 1.25 GiB of HBM per device.

v0:
```python
import jax
import jax.numpy as jnp
from jax import lax
from jax.sharding import PartitionSpec as P

LN_EPS = 1.0e-5
NEG_BIG = -1.0e30


def layer_norm(residual, ln_gain):
    resid_f32 = residual.astype(jnp.float32)
    row_mean = jnp.mean(resid_f32, axis=-1, keepdims=True)
    centered = resid_f32 - row_mean
    row_var = jnp.mean(centered * centered, axis=-1, keepdims=True)
    return (centered * lax.rsqrt(row_var + LN_EPS) * ln_gain).astype(jnp.bfloat16)


def causal_attention(query_blk, key_blk, value_blk, query_start):
    head_dim = query_blk.shape[-1]
    scores = jnp.einsum('bqhe,bkhe->bhqk', query_blk, key_blk, preferred_element_type=jnp.float32) * head_dim ** -0.5
    query_pos = query_start + jnp.arange(query_blk.shape[1])
    key_pos = jnp.arange(key_blk.shape[1])
    scores = jnp.where(query_pos[:, None] >= key_pos[None, :], scores, NEG_BIG)
    attn_probs = jax.nn.softmax(scores, axis=-1).astype(jnp.bfloat16)
    return jnp.einsum('bhqk,bkhe->bqhe', attn_probs, value_blk, preferred_element_type=jnp.float32).astype(jnp.bfloat16)


def solution(mesh):
    def layer_stack(x_local, ln1_gain, w_qkv, w_out, ln2_gain, w_up, w_down):
        residual = x_local
        head_dim = w_qkv.shape[3] // 3
        for layer_idx in range(w_qkv.shape[0]):
            normed = layer_norm(residual, ln1_gain[layer_idx])
            normed_all = lax.all_gather(normed, 'tp', axis=1, tiled=True)
            qkv_all = jnp.einsum('bsd,dhe->bshe', normed_all, w_qkv[layer_idx], preferred_element_type=jnp.float32).astype(jnp.bfloat16)
            attended = causal_attention(qkv_all[..., :head_dim], qkv_all[..., head_dim:2 * head_dim], qkv_all[..., 2 * head_dim:], 0)
            part_sum = jnp.einsum('bshe,hed->bsd', attended, w_out[layer_idx], preferred_element_type=jnp.float32).astype(jnp.bfloat16)
            reduced = lax.psum_scatter(part_sum, 'tp', scatter_dimension=1, tiled=True)
            residual = (residual.astype(jnp.float32) + reduced.astype(jnp.float32)).astype(jnp.bfloat16)
            normed = layer_norm(residual, ln2_gain[layer_idx])
            normed_all = lax.all_gather(normed, 'tp', axis=1, tiled=True)
            hidden = jax.nn.gelu(jnp.einsum('bsd,df->bsf', normed_all, w_up[layer_idx], preferred_element_type=jnp.float32), approximate=True).astype(jnp.bfloat16)
            part_sum = jnp.einsum('bsf,fd->bsd', hidden, w_down[layer_idx], preferred_element_type=jnp.float32).astype(jnp.bfloat16)
            reduced = lax.psum_scatter(part_sum, 'tp', scatter_dimension=1, tiled=True)
            residual = (residual.astype(jnp.float32) + reduced.astype(jnp.float32)).astype(jnp.bfloat16)
        return residual

    return jax.shard_map(layer_stack, mesh=mesh, in_specs=(P('dp', 'tp', None), P(), P(None, None, 'tp', None), P(None, 'tp', None, None), P(), P(None, None, 'tp'), P(None, 'tp', None)), out_specs=P('dp', 'tp', None), check_vma=False)
```

profile of v0, /device:TPU:0, one launch (start us, length us, event | category | flops | bytes accessed | tf_op | source)
XLA Modules:
  0.0 300.6 jit_solution(7643065896908407959)
XLA Ops:
  6.5 0.0 all-gather.5.cloned.1.call-start
  6.5 1.1 convert_reduce_fusion.3
  7.7 1.2 fusion.135
  8.9 0.9 fusion.162
  9.8 1.9 fusion.137
  11.7 0.0 all-gather.5.cloned.1.call-update
  11.7 0.0 reduce-scatter.5.cloned.1.call-start
  11.8 18.1 %all-gather.5.cloned.1.call-done = bf16[1,128,5120]{2,1,0:T(8,128)(2,1)} async-done(((bf16[1,32,5120]{2,1,0:T(8,128)(2,1)}), bf16[1,128,5120]{2,1,0:T(8,128)(2,1)}) %all-gather.5.cloned.1.call-update) | async-done | bytes 1310736 | tf_op jit(solution)/shard_map/all_gather | solution.py:34
  29.9 15.5 %fusion.95 = bf16[1,128,10,384]{3,1,2,0:T(8,128)(2,1)S(1)} fusion(bf16[2,5120,10,384]{3,1,2,0:T(8,128)(2,1)} %param.9, bf16[1,128,5120]{2,1,0:T(8,128)(2,1)} %all-gather.5.cloned.1.call-done), kind=kOutput, calls=%fused_computation.59 | convolution fusion | flops 5033656320 | bytes 41615360 | tf_op jit(solution)/shard_map/bsd,dhe->bshe/dot_general | solution.py:35
  45.3 0.4 fusion.114
  45.7 0.1 fusion.163
  45.9 0.0 copy-start.1
  45.9 0.0 copy-start
  45.9 8.0 %fusion.44 = bf16[1,128,5120]{2,1,0:T(8,128)(2,1)} fusion(bf16[2,10,128,5120]{3,2,1,0:T(8,128)(2,1)} %param.10, bf16[1,128,10,384]{3,1,2,0:T(8,128)(2,1)S(1)} %fusion.95, f32[10,128]{1,0:T(8,128)S(1)} %fusion.163, f32[10,128,128]{1,2,0:T(8,128)S(1)} %fusion.114), kind=kOutput, calls=%fused_computation.32 | convolution fusion | flops 1720976768 | bytes 16061440 | tf_op jit(solution)/shard_map/bshe,hed->bsd/dot_general | solution.py:37
  53.9 0.0 reduce-scatter.5.cloned.1.call-update
  53.9 0.0 all-gather.7.cloned.1.call-start
  54.0 0.0 copy-done.1
  54.0 20.8 %reduce-scatter.5.cloned.1.call-done = bf16[1,32,5120]{2,1,0:T(8,128)(2,1)} async-done(((bf16[1,128,5120]{2,1,0:T(8,128)(2,1)}), bf16[1,32,5120]{2,1,0:T(8,128)(2,1)}) %reduce-scatter.5.cloned.1.call-update) | async-done | bytes 327696 | tf_op jit(solution)/shard_map/reduce_scatter | solution.py:38
  74.8 0.0 copy-done
  74.8 1.2 convert_reduce_fusion.2
  76.0 0.3 fusion.132
  76.3 0.9 fusion.134
  77.2 0.0 all-gather.7.cloned.1.call-update
  77.2 0.0 reduce-scatter.7.cloned.1.call-start
  77.3 15.3 %all-gather.7.cloned.1.call-done = bf16[1,128,5120]{2,1,0:T(8,128)(2,1)} async-done(((bf16[1,32,5120]{2,1,0:T(8,128)(2,1)}), bf16[1,128,5120]{2,1,0:T(8,128)(2,1)}) %all-gather.7.cloned.1.call-update) | async-done | bytes 1310736 | tf_op jit(solution)/shard_map/all_gather | solution.py:41
  92.5 19.4 %fusion.65.clone.5 = bf16[128,5120]{1,0:T(8,128)(2,1)S(1)} fusion(bf16[2,5120,5120]{2,1,0:T(8,128)(2,1)} %param.12, bf16[1,128,5120]{2,1,0:T(8,128)(2,1)} %all-gather.7.cloned.1.call-done), kind=kOutput, calls=%fused_computation.45.clone.clone.clone.2 | convolution fusion | flops 6716784640 | bytes 55050240 | tf_op jit(solution)/shard_map/bsd,df->bsf/dot_general | solution.py:42
  111.9 19.3 %fusion.53 = bf16[1,128,5120]{2,1,0:T(8,128)(2,1)} fusion(bf16[2,5120,5120]{2,1,0:T(8,128)(2,1)} %param.13, bf16[128,5120]{1,0:T(8,128)(2,1)S(1)} %fusion.65.clone.5), kind=kOutput, calls=%fused_computation.35 | convolution fusion | flops 6711541760 | bytes 55050240 | tf_op jit(solution)/shard_map/bsf,fd->bsd/dot_general | solution.py:43
  131.2 0.0 reduce-scatter.7.cloned.1.call-update
  131.2 0.0 all-gather.9.cloned.1.call-start
  131.3 20.9 %reduce-scatter.7.cloned.1.call-done = bf16[1,32,5120]{2,1,0:T(8,128)(2,1)} async-done(((bf16[1,128,5120]{2,1,0:T(8,128)(2,1)}), bf16[1,32,5120]{2,1,0:T(8,128)(2,1)}) %reduce-scatter.7.cloned.1.call-update) | async-done | bytes 327696 | tf_op jit(solution)/shard_map/reduce_scatter | solution.py:44
  152.1 1.2 convert_reduce_fusion.1
  153.3 0.3 fusion.129
  153.6 0.9 fusion.131
  154.5 0.0 all-gather.9.cloned.1.call-update
  154.5 0.2 reduce-scatter.9.cloned.1.call-start
  154.8 15.1 %all-gather.9.cloned.1.call-done = bf16[1,128,5120]{2,1,0:T(8,128)(2,1)} async-done(((bf16[1,32,5120]{2,1,0:T(8,128)(2,1)}), bf16[1,128,5120]{2,1,0:T(8,128)(2,1)}) %all-gather.9.cloned.1.call-update) | async-done | bytes 1310736 | tf_op jit(solution)/shard_map/all_gather | solution.py:34
  169.8 15.5 %fusion.92 = bf16[1,128,10,384]{3,1,2,0:T(8,128)(2,1)S(1)} fusion(bf16[2,5120,10,384]{3,1,2,0:T(8,128)(2,1)} %param.9, bf16[1,128,5120]{2,1,0:T(8,128)(2,1)} %all-gather.9.cloned.1.call-done), kind=kOutput, calls=%fused_computation.58 | convolution fusion | flops 5033656320 | bytes 41615360 | tf_op jit(solution)/shard_map/bsd,dhe->bshe/dot_general | solution.py:35
  185.3 0.4 fusion.115
  185.7 0.1 fusion.164
  185.8 8.0 %fusion.47 = bf16[1,128,5120]{2,1,0:T(8,128)(2,1)} fusion(bf16[2,10,128,5120]{3,2,1,0:T(8,128)(2,1)} %param.10, bf16[1,128,10,384]{3,1,2,0:T(8,128)(2,1)S(1)} %fusion.92, f32[10,128]{1,0:T(8,128)S(1)} %fusion.164, f32[10,128,128]{1,2,0:T(8,128)S(1)} %fusion.115), kind=kOutput, calls=%fused_computation.33 | convolution fusion | flops 1720976768 | bytes 16061440 | tf_op jit(solution)/shard_map/bshe,hed->bsd/dot_general | solution.py:37
  193.8 0.0 reduce-scatter.9.cloned.1.call-update
  193.8 0.0 all-gather.11.cloned.1.call-start
  193.9 20.8 %reduce-scatter.9.cloned.1.call-done = bf16[1,32,5120]{2,1,0:T(8,128)(2,1)} async-done(((bf16[1,128,5120]{2,1,0:T(8,128)(2,1)}), bf16[1,32,5120]{2,1,0:T(8,128)(2,1)}) %reduce-scatter.9.cloned.1.call-update) | async-done | bytes 327696 | tf_op jit(solution)/shard_map/reduce_scatter | solution.py:38
  214.7 1.2 convert_reduce_fusion
  215.9 0.3 fusion.126
  216.2 0.9 fusion.128
  217.1 0.0 all-gather.11.cloned.1.call-update
  217.1 0.0 reduce-scatter.11.cloned.1.call-start
  217.2 15.3 %all-gather.11.cloned.1.call-done = bf16[1,128,5120]{2,1,0:T(8,128)(2,1)} async-done(((bf16[1,32,5120]{2,1,0:T(8,128)(2,1)}), bf16[1,128,5120]{2,1,0:T(8,128)(2,1)}) %all-gather.11.cloned.1.call-update) | async-done | bytes 1310736 | tf_op jit(solution)/shard_map/all_gather | solution.py:41
  232.5 19.4 %fusion.79.clone.5 = bf16[128,5120]{1,0:T(8,128)(2,1)S(1)} fusion(bf16[2,5120,5120]{2,1,0:T(8,128)(2,1)} %param.12, bf16[1,128,5120]{2,1,0:T(8,128)(2,1)} %all-gather.11.cloned.1.call-done), kind=kOutput, calls=%fused_computation.53.clone.clone.clone.2 | convolution fusion | flops 6716784640 | bytes 55050240 | tf_op jit(solution)/shard_map/bsd,df->bsf/dot_general | solution.py:42
  251.8 19.3 %fusion.50 = bf16[1,128,5120]{2,1,0:T(8,128)(2,1)} fusion(bf16[2,5120,5120]{2,1,0:T(8,128)(2,1)} %param.13, bf16[128,5120]{1,0:T(8,128)(2,1)S(1)} %fusion.79.clone.5), kind=kOutput, calls=%fused_computation.34 | convolution fusion | flops 6711541760 | bytes 55050240 | tf_op jit(solution)/shard_map/bsf,fd->bsd/dot_general | solution.py:43
  271.1 0.0 reduce-scatter.11.cloned.1.call-update
  271.1 20.9 %reduce-scatter.11.cloned.1.call-done = bf16[1,32,5120]{2,1,0:T(8,128)(2,1)} async-done(((bf16[1,128,5120]{2,1,0:T(8,128)(2,1)}), bf16[1,32,5120]{2,1,0:T(8,128)(2,1)}) %reduce-scatter.11.cloned.1.call-update) | async-done | bytes 327696 | tf_op jit(solution)/shard_map/reduce_scatter | solution.py:44
  292.0 1.8 fusion.141
  (10 shorter events, 0.1 us)
Async XLA Ops:
  6.5 23.3 %all-gather.5.cloned.1.call-start = ((), (), s32[]{:S(2)}) async-start(), calls=%async_computation.4 | async-start | bytes 1638400 | tf_op jit(solution)/shard_map/all_gather | solution.py:34
  11.7 63.1 %reduce-scatter.5.cloned.1.call-start = ((), (), s32[]{:S(2)}) async-start(), calls=%async_computation.5 | async-start | bytes 1638400 | tf_op jit(solution)/shard_map/reduce_scatter | solution.py:38
  45.9 8.1 %copy-start.1 = (f32[2,5120]{1,0:T(2,128)S(1)}, f32[2,5120]{1,0:T(2,128)}, u32[]{:S(2)}) copy-start(f32[2,5120]{1,0:T(2,128)} %param.11) | copy-start | bytes 122884
  45.9 28.9 %copy-start = (bf16[1,32,5120]{2,1,0:T(8,128)(2,1)S(1)}, bf16[1,32,5120]{2,1,0:T(8,128)(2,1)}, u32[]{:S(2)}) copy-start(bf16[1,32,5120]{2,1,0:T(8,128)(2,1)} %param.7) | copy-start | bytes 983044
  53.9 38.6 %all-gather.7.cloned.1.call-start = ((), (), s32[]{:S(2)}) async-start(), calls=%async_computation.6 | async-start | bytes 1638400 | tf_op jit(solution)/shard_map/all_gather | solution.py:41
  77.2 74.9 %reduce-scatter.7.cloned.1.call-start = ((), (), s32[]{:S(2)}) async-start(), calls=%async_computation.7 | async-start | bytes 1638400 | tf_op jit(solution)/shard_map/reduce_scatter | solution.py:44
  131.2 38.6 %all-gather.9.cloned.1.call-start = ((), (), s32[]{:S(2)}) async-start(), calls=%async_computation.8 | async-start | bytes 1638400 | tf_op jit(solution)/shard_map/all_gather | solution.py:34
  154.5 60.2 %reduce-scatter.9.cloned.1.call-start = ((), (), s32[]{:S(2)}) async-start(), calls=%async_computation.9 | async-start | bytes 1638400 | tf_op jit(solution)/shard_map/reduce_scatter | solution.py:38
  193.8 38.6 %all-gather.11.cloned.1.call-start = ((), (), s32[]{:S(2)}) async-start(), calls=%async_computation.10 | async-start | bytes 1638400 | tf_op jit(solution)/shard_map/all_gather | solution.py:41
  217.1 74.9 %reduce-scatter.11.cloned.1.call-start = ((), (), s32[]{:S(2)}) async-start(), calls=%async_computation.11 | async-start | bytes 1638400 | tf_op jit(solution)/shard_map/reduce_scatter | solution.py:44
Sparse Core Ops, SparseCore 0:
  11.8 17.9 all-gather.4
  54.0 20.7 reduce-scatter.4
  77.3 15.1 all-gather.6
  131.3 20.7 reduce-scatter.6
  154.7 15.1 all-gather.8
  194.0 20.7 reduce-scatter.8
  217.2 15.1 all-gather.10
  271.2 20.7 reduce-scatter.10
where the time goes:
time: 301 us
  waiting for transfers between devices  147 us (49%)
  matrix products  125 us (42%)
  between operations  13.6 us (5%)
  other arithmetic  13.4 us (4%)
    reduce_scatter x4, waiting for transfers between devices, layer_stack(): reduced = lax.psum_scatter(part_sum, 'tp', scatter_dimension=1, tiled=True)  83.4 us
    all_gather x4, waiting for transfers between devices, layer_stack(): normed_all = lax.all_gather(normed, 'tp', axis=1, tiled=True)  63.7 us
    dot_general x2, matrix products, layer_stack(): jnp.einsum('bsd,df->bsf', normed_all, w_up[layer_idx], preferred_element_...  38.7 us
    dot_general x2, matrix products, layer_stack(): jnp.einsum('bsf,fd->bsd', hidden, w_down[layer_idx], preferred_element_ty...  38.6 us
    dot_general x2, matrix products, layer_stack(): jnp.einsum('bsd,dhe->bshe', normed_all, w_qkv[layer_idx], preferred_eleme...  31 us
    dot_general x2, matrix products, layer_stack(): jnp.einsum('bshe,hed->bsd', attended, w_out[layer_idx], preferred_element...  16 us
  transfers between devices with their start and end apart: 8, of which 8 were waited for; matrix products, arithmetic and copies ran while one was open for 0% of the time, Pallas kernels for 0%

commit v1 on v0

v1 whole, which is shorter than its diff:
```python
import functools

import jax
import jax.numpy as jnp
from jax import lax
from jax.experimental import pallas as pl
from jax.experimental.pallas import tpu as pltpu
from jax.sharding import PartitionSpec as P

LN_EPS = 1.0e-5
NEG_BIG = -1.0e30
MESH = pl.DeviceIdType.MESH

TP = 4
SEQ = 128
ROWS = SEQ // TP
D = 5120
C = 1280
NC = D // C
HEADS = 10
HD = 128
SLOTS = 16
LAYERS = 2
NW = 256


def stack_kernel(x_hbm, g1_ref, wqkv_hbm, wout_hbm, g2_ref, wup_hbm, wdown_hbm, y_hbm,
                 ring, a_all, hid, acc, att, xres, p_snd, p_rcv, q_snd, q_rcv,
                 ring_sem, x_sem, ag_s, ag_r, p_s, p_r, q_s, q_r):
    me = lax.axis_index('tp')
    partner = me + 1 - 2 * lax.rem(me, 2)
    cross = lax.rem(me + 2, TP)
    diag = lax.rem(partner + 2, TP)

    def tile(w, layer, row, col, slot):
        rows = pl.ds(pl.multiple_of(row * C, C), C)
        cols = pl.ds(pl.multiple_of(col * C, C), C)
        return pltpu.make_async_copy(w.at[layer, rows, cols], ring.at[slot], ring_sem.at[slot])

    def start_qkv(layer, i):
        j, s = i // 3, i % 3
        rows = pl.ds(j * C, C)
        pieces, col = [], 0
        for head in range(HEADS):
            lo, hi = head * 3 * HD, (head + 1) * 3 * HD
            a, b = max(lo, s * C), min(hi, (s + 1) * C)
            if a < b:
                pieces.append((head, a - lo, b - a, a - s * C))
        for head, src, width, dst in pieces:
            pltpu.make_async_copy(wqkv_hbm.at[layer, head, rows, pl.ds(src, width)],
                                  ring.at[i, :, pl.ds(dst, width)], ring_sem.at[i]).start(priority=1)

    def start_attention_tile(layer, i):
        if i < 12:
            start_qkv(layer, i)
        else:
            tile(wout_hbm, layer, 0, i - 12, i).start(priority=1)

    def start_up(layer, i):
        tile(wup_hbm, layer, i // NC, lax.rem(i, NC), i).start(priority=1)

    def start_down(layer, i):
        tile(wdown_hbm, layer, lax.rem(i, NC), i // NC, i).start(priority=1)

    def wait_tile(slot):
        tile(wup_hbm, 0, 0, 0, slot).wait()

    def step(lhs, slot, dst, first, finish=None):
        lhs_val = lhs.reshape(SEQ, C)
        for n in range(C // NW):
            cols = pl.ds(n * NW, NW)
            part = jnp.dot(lhs_val, ring[slot, :, cols], preferred_element_type=jnp.float32)
            if not first:
                part = part + acc[dst, :, :, cols].reshape(SEQ, NW)
            if finish is None:
                acc[dst, :, :, cols] = part.reshape(TP, ROWS, NW)
            else:
                finish(part, cols)

    def remote(src, dst, send_sem, recv_sem, peer):
        return pltpu.make_async_remote_copy(src_ref=src, dst_ref=dst, send_sem=send_sem, recv_sem=recv_sem,
                                            device_id={'tp': peer}, device_id_type=MESH)

    def ag_copy(j, kind):
        block, peer = ((me, partner), (me, cross), (cross, partner))[kind]
        return remote(a_all.at[j, block], a_all.at[j, block], ag_s.at[kind, j], ag_r.at[kind, j], peer)

    def ag_wait(j, kind):
        block = (partner, cross, diag)[kind]
        remote(a_all.at[j, block], a_all.at[j, block], ag_s.at[kind, j], ag_r.at[kind, j], partner).wait_recv()

    def norm_and_send(g_ref, layer):
        total = jnp.zeros((ROWS, 1), jnp.float32)
        for j in range(NC):
            total += jnp.sum(xres[j].astype(jnp.float32), axis=-1, keepdims=True)
        mean = total / D
        total = jnp.zeros((ROWS, 1), jnp.float32)
        for j in range(NC):
            centered = xres[j].astype(jnp.float32) - mean
            total += jnp.sum(centered * centered, axis=-1, keepdims=True)
        scale = lax.rsqrt(total / D + LN_EPS)
        for j in range(NC):
            gain = g_ref[pl.ds(layer, 1), pl.ds(j * C, C)]
            a_all[j, me] = ((xres[j].astype(jnp.float32) - mean) * scale * gain).astype(jnp.bfloat16)
            ag_copy(j, 1).start()
            ag_copy(j, 0).start()

    def forward(j):
        ag_wait(j, 1)
        ag_copy(j, 2).start()

    def ag_drain():
        for j in range(NC):
            for kind in range(3):
                ag_copy(j, kind).wait_send()

    def rs_p(q):
        return remote(p_snd.at[q], p_rcv.at[q], p_s.at[q], p_r.at[q], partner)

    def rs_q(q):
        return remote(q_snd.at[q], q_rcv.at[q], q_s.at[q], q_r.at[q], cross)

    def rs_a(q):
        p_snd[q, 0] = acc[q, partner].astype(jnp.bfloat16)
        p_snd[q, 1] = acc[q, diag].astype(jnp.bfloat16)
        rs_p(q).start()

    def rs_b(q):
        rs_p(q).wait_recv()
        q_snd[q] = (acc[q, cross] + p_rcv[q, 1].astype(jnp.float32)).astype(jnp.bfloat16)
        rs_q(q).start()

    def rs_c(q):
        rs_q(q).wait_recv()
        total = acc[q, me] + p_rcv[q, 0].astype(jnp.float32) + q_rcv[q].astype(jnp.float32)
        xres[q] = (xres[q].astype(jnp.float32) + total).astype(jnp.bfloat16)

    def rs_drain():
        for q in range(NC):
            rs_p(q).wait_send()
            rs_q(q).wait_send()

    def attention():
        rows = lax.broadcasted_iota(jnp.int32, (SEQ, SEQ), 0)
        cols = lax.broadcasted_iota(jnp.int32, (SEQ, SEQ), 1)
        causal = rows >= cols

        def part(block):
            third, col = block * HD // C, block * HD % C
            return acc[third, :, :, pl.ds(col, HD)].reshape(SEQ, HD).astype(jnp.bfloat16)

        for head in range(HEADS):
            query, key, value = part(3 * head), part(3 * head + 1), part(3 * head + 2)
            scores = lax.dot_general(query, key, (((1,), (1,)), ((), ())), preferred_element_type=jnp.float32)
            scores = jnp.where(causal, scores * HD ** -0.5, NEG_BIG)
            probs = jnp.exp(scores - jnp.max(scores, axis=-1, keepdims=True))
            probs = (probs / jnp.sum(probs, axis=-1, keepdims=True)).astype(jnp.bfloat16)
            out = jnp.dot(probs, value, preferred_element_type=jnp.float32)
            att[:, pl.ds(head * HD, HD)] = out.astype(jnp.bfloat16)

    x_copies = [pltpu.make_async_copy(x_hbm.at[0, :, pl.ds(j * C, C)], xres.at[j], x_sem) for j in range(NC)]
    for copy in x_copies:
        copy.start()
    for i in range(SLOTS):
        start_attention_tile(0, i)
    barrier = pltpu.get_barrier_semaphore()
    for peer in (partner, cross):
        pl.semaphore_signal(barrier, inc=1, device_id={'tp': peer}, device_id_type=MESH)
    pl.semaphore_wait(barrier, 2)
    for copy in x_copies:
        copy.wait()

    def loop(lo, hi, body):
        lax.fori_loop(lo, hi, lambda i, carry: (body(i), carry)[1], 0)

    def layer_body(layer):
        norm_and_send(g1_ref, layer)
        forward(0)

        def qkv_chunk(j, first):
            ag_wait(j, 0)
            ag_wait(j, 2)

            def third(s):
                i = 3 * j + s
                wait_tile(i)
                step(a_all[j], i, s, first)
                start_up(layer, i)

            third(0)

            @pl.when(j < NC - 1)
            def _():
                forward(j + 1)

            loop(1, 3, third)

        qkv_chunk(0, True)
        loop(1, NC, lambda j: qkv_chunk(j, False))
        ag_drain()
        attention()

        def out_quarter(q):
            wait_tile(12 + q)
            step(att[...], 12 + q, q, True)
            start_up(layer, 12 + q)
            rs_a(q)

            @pl.when(q >= 2)
            def _():
                rs_b(q - 2)

        loop(0, NC, out_quarter)
        rs_b(2)
        rs_b(3)
        loop(0, NC, rs_c)
        rs_drain()

        norm_and_send(g2_ref, layer)
        forward(0)

        def up_chunk(j, first, last):
            ag_wait(j, 0)
            ag_wait(j, 2)

            def quarter(q):
                i = NC * j + q

                def finish(part, cols):
                    hid[q, :, cols] = jax.nn.gelu(part, approximate=True).astype(jnp.bfloat16)

                wait_tile(i)
                step(a_all[j], i, q, first, finish if last else None)
                start_down(layer, i)

            quarter(0)
            if not last:
                forward(j + 1)
            loop(1, NC, quarter)

        up_chunk(0, True, False)
        loop(1, NC - 1, lambda j: up_chunk(j, False, False))
        up_chunk(NC - 1, False, True)
        ag_drain()

        def next_tiles(i):
            @pl.when(layer < LAYERS - 1)
            def _():
                for k in range(SLOTS):
                    @pl.when(i == k)
                    def _():
                        start_attention_tile(layer + 1, k)

        def down_quarter(q):
            def chunk(j, first):
                i = NC * q + j
                wait_tile(i)
                step(hid[j], i, q, first)
                next_tiles(i)

            chunk(0, True)
            chunk(1, False)

            @pl.when(q >= 1)
            def _():
                rs_b(q - 1)

            loop(2, NC, lambda j: chunk(j, False))
            rs_a(q)

        loop(0, NC, down_quarter)
        rs_b(NC - 1)
        loop(0, NC, rs_c)
        rs_drain()

    loop(0, LAYERS, layer_body)
    y_copies = [pltpu.make_async_copy(xres.at[j], y_hbm.at[0, :, pl.ds(j * C, C)], x_sem) for j in range(NC)]
    for copy in y_copies:
        copy.start()
    for copy in y_copies:
        copy.wait()


def solution(mesh):
    def layer_stack(x_local, ln1_gain, w_qkv, w_out, ln2_gain, w_up, w_down):
        w_qkv = jnp.transpose(w_qkv, (0, 2, 1, 3))
        w_out = w_out.reshape(LAYERS, HEADS * HD, D)
        hbm = pl.BlockSpec(memory_space=pl.ANY)
        vmem = pl.BlockSpec(memory_space=pltpu.VMEM)
        weight_bytes = 2 * LAYERS * (3 * C * D + C * D + 2 * D * D)
        return pl.pallas_call(
            stack_kernel,
            out_shape=jax.ShapeDtypeStruct(x_local.shape, jnp.bfloat16),
            in_specs=[hbm, vmem, hbm, hbm, vmem, hbm, hbm],
            out_specs=hbm,
            scratch_shapes=[
                pltpu.VMEM((SLOTS, C, C), jnp.bfloat16),
                pltpu.VMEM((NC, TP, ROWS, C), jnp.bfloat16),
                pltpu.VMEM((NC, SEQ, C), jnp.bfloat16),
                pltpu.VMEM((NC, TP, ROWS, C), jnp.float32),
                pltpu.VMEM((SEQ, C), jnp.bfloat16),
                pltpu.VMEM((NC, ROWS, C), jnp.bfloat16),
                pltpu.VMEM((NC, 2, ROWS, C), jnp.bfloat16),
                pltpu.VMEM((NC, 2, ROWS, C), jnp.bfloat16),
                pltpu.VMEM((NC, ROWS, C), jnp.bfloat16),
                pltpu.VMEM((NC, ROWS, C), jnp.bfloat16),
                pltpu.SemaphoreType.DMA((SLOTS,)),
                pltpu.SemaphoreType.DMA,
                pltpu.SemaphoreType.DMA((3, NC)),
                pltpu.SemaphoreType.DMA((3, NC)),
                pltpu.SemaphoreType.DMA((NC,)),
                pltpu.SemaphoreType.DMA((NC,)),
                pltpu.SemaphoreType.DMA((NC,)),
                pltpu.SemaphoreType.DMA((NC,)),
            ],
            compiler_params=pltpu.CompilerParams(collective_id=0, has_side_effects=True, vmem_limit_bytes=67_043_328),
            cost_estimate=pl.CostEstimate(flops=SEQ * weight_bytes, bytes_accessed=weight_bytes, transcendentals=0),
        )(x_local, ln1_gain, w_qkv, w_out, ln2_gain, w_up, w_down)

    return jax.shard_map(layer_stack, mesh=mesh, in_specs=(P('dp', 'tp', None), P(), P(None, None, 'tp', None), P(None, 'tp', None, None), P(), P(None, None, 'tp'), P(None, 'tp', None)), out_specs=P('dp', 'tp', None), check_vma=False)
```

time: 301 us -> 124 us (0.41)
  waiting for transfers between devices: 147 us -> 0 us
  matrix products: 125 us -> 0 us
  Pallas kernels: 0 us -> 122 us
  between operations: 13.6 us -> 0.01 us
  other arithmetic: 13.4 us -> 0 us
    dot_general x10 -> x0, matrix products: 125 us -> none  [the longest x2 38.7 us: layer_stack(): jnp.einsum('bsd,df->bsf', normed_all, w_up[layer_idx], preferred_element_...]
    pallas_call x0 -> x1, Pallas kernels: none -> 122 us  [layer_stack(): pl.pallas_call(stack_kernel, out_shape=jax.ShapeDtypeStruct(x_local.shape...]
    reduce_scatter x4 -> x0, waiting for transfers between devices: 83.4 us -> none  [layer_stack(): reduced = lax.psum_scatter(part_sum, 'tp', scatter_dimension=1, tiled=True)]
    all_gather x4 -> x0, waiting for transfers between devices: 63.7 us -> none  [layer_stack(): normed_all = lax.all_gather(normed, 'tp', axis=1, tiled=True)]
    reduce_sum x8 -> x0, other arithmetic: 6.72 us -> none  [the longest x4 4.65 us: layer_norm(): row_mean = jnp.mean(resid_f32, axis=-1, keepdims=True)]
    convert_element_type x5 -> x0, other arithmetic: 6.33 us -> none  [the longest x4 4.56 us: layer_norm(): (centered * lax.rsqrt(row_var + LN_EPS) * ln_gain).astype(jnp.bfloat16)]
  transfers between devices with their start and end apart: 8 -> 0, of which waited for: 8 -> 0; matrix products, arithmetic and copies ran while one was open for 0% -> 0% of each run, Pallas kernels for 0% -> 0%
where the time goes in v1:
time: 124 us
  Pallas kernels  122 us (98%)
  local copies, waits for them, and re-layouts  1.72 us (1%)
    pallas_call x1, Pallas kernels, layer_stack(): pl.pallas_call(stack_kernel, out_shape=jax.ShapeDtypeStruct(x_local.shape...  122 us

profile of v1, /device:TPU:0, one launch (start us, length us, event | category | flops | bytes accessed | tf_op | source)
XLA Modules:
  0.0 123.7 jit_solution(5219771960298472787)
XLA Ops:
  0.0 121.9 %shard_map.73 = bf16[1,32,5120]{2,1,0:T(8,128)(2,1)} custom-call(bf16[1,32,5120]{2,1,0:T(8,128)(2,1)} %x_hbm.1, f32[2,5120]{1,0:T(2,128)} %g1_ref.1, bf16[2,10,5120,384]{3,2,1,0:T(8,128)(2,1)} %bitcast.wqkv_hbm, bf16[2,1280,5120]{2,1,0:T(8,128)(2,1)} %bitcast.2, f32[2,5120]{1,0:T(2,128)} %g2_ref.1, bf16[2,5120,5120]{2,1,0:T(8,128)(2,1)} %wup_hbm.1, ...), custom_call_target="tpu_custom_call" | custom-call | flops 40265318400 | bytes 314572800 | tf_op jit(solution)/shard_map/pallas_call | solution.py:291
  121.9 1.7 %copy.9 = bf16[1,32,5120]{2,1,0:T(8,128)(2,1)} copy(bf16[1,32,5120]{2,1,0:T(8,128)(2,1)} %shard_map.73) | data formatting | bytes 655360

commit v2 on v1

--- a/solution.py
+++ b/solution.py
@@ -24,9 +24,9 @@
 NW = 256
 
 
-def stack_kernel(x_hbm, g1_ref, wqkv_hbm, wout_hbm, g2_ref, wup_hbm, wdown_hbm, y_hbm,
-                 ring, a_all, hid, acc, att, xres, p_snd, p_rcv, q_snd, q_rcv,
-                 ring_sem, x_sem, ag_s, ag_r, p_s, p_r, q_s, q_r):
+def stack_kernel(x_hbm, g1_hbm, wqkv_hbm, wout_hbm, g2_hbm, wup_hbm, wdown_hbm, y_hbm,
+                 ring, a_all, hid, acc, att, s_buf, p_buf, xres, p_snd, p_rcv, q_snd, q_rcv, g1_ref, g2_ref,
+                 ring_sem, x_sem, g_sem, ag_s, ag_r, p_s, p_r, q_s, q_r):
     me = lax.axis_index('tp')
     partner = me + 1 - 2 * lax.rem(me, 2)
     cross = lax.rem(me + 2, TP)
@@ -65,17 +65,20 @@
     def wait_tile(slot):
         tile(wup_hbm, 0, 0, 0, slot).wait()
 
-    def step(lhs, slot, dst, first, finish=None):
-        lhs_val = lhs.reshape(SEQ, C)
-        for n in range(C // NW):
-            cols = pl.ds(n * NW, NW)
-            part = jnp.dot(lhs_val, ring[slot, :, cols], preferred_element_type=jnp.float32)
-            if not first:
-                part = part + acc[dst, :, :, cols].reshape(SEQ, NW)
-            if finish is None:
-                acc[dst, :, :, cols] = part.reshape(TP, ROWS, NW)
-            else:
-                finish(part, cols)
+    def block(jobs):
+        for pairs, dst, add, finish in jobs:
+            for n in range(C // NW):
+                cols = pl.ds(n * NW, NW)
+                part = None
+                for lhs, slot in pairs:
+                    term = jnp.dot(lhs(), ring[slot, :, cols], preferred_element_type=jnp.float32)
+                    part = term if part is None else part + term
+                if add:
+                    part = part + acc[dst, :, :, cols].reshape(SEQ, NW)
+                if finish is None:
+                    acc[dst, :, :, cols] = part.reshape(TP, ROWS, NW)
+                else:
+                    finish(part, dst, cols)
 
     def remote(src, dst, send_sem, recv_sem, peer):
         return pltpu.make_async_remote_copy(src_ref=src, dst_ref=dst, send_sem=send_sem, recv_sem=recv_sem,
@@ -141,25 +144,30 @@
             rs_q(q).wait_send()
 
     def attention():
-        rows = lax.broadcasted_iota(jnp.int32, (SEQ, SEQ), 0)
-        cols = lax.broadcasted_iota(jnp.int32, (SEQ, SEQ), 1)
-        causal = rows >= cols
+        keys = lax.broadcasted_iota(jnp.int32, (SEQ, SEQ), 0)
+        queries = lax.broadcasted_iota(jnp.int32, (SEQ, SEQ), 1)
+        causal = queries >= keys
 
         def part(block):
             third, col = block * HD // C, block * HD % C
             return acc[third, :, :, pl.ds(col, HD)].reshape(SEQ, HD).astype(jnp.bfloat16)
 
         for head in range(HEADS):
-            query, key, value = part(3 * head), part(3 * head + 1), part(3 * head + 2)
-            scores = lax.dot_general(query, key, (((1,), (1,)), ((), ())), preferred_element_type=jnp.float32)
-            scores = jnp.where(causal, scores * HD ** -0.5, NEG_BIG)
-            probs = jnp.exp(scores - jnp.max(scores, axis=-1, keepdims=True))
-            probs = (probs / jnp.sum(probs, axis=-1, keepdims=True)).astype(jnp.bfloat16)
-            out = jnp.dot(probs, value, preferred_element_type=jnp.float32)
+            query, key = part(3 * head), part(3 * head + 1)
+            scores = lax.dot_general(key, query, (((1,), (1,)), ((), ())), preferred_element_type=jnp.float32)
+            s_buf[head] = jnp.where(causal, scores * HD ** -0.5, NEG_BIG)
+        for head in range(HEADS):
+            scores = s_buf[head]
+            probs = jnp.exp(scores - jnp.max(scores, axis=0, keepdims=True))
+            p_buf[head] = (probs / jnp.sum(probs, axis=0, keepdims=True)).astype(jnp.bfloat16)
+        for head in range(HEADS):
+            out = lax.dot_general(p_buf[head], part(3 * head + 2), (((0,), (0,)), ((), ())),
+                                  preferred_element_type=jnp.float32)
             att[:, pl.ds(head * HD, HD)] = out.astype(jnp.bfloat16)
 
-    x_copies = [pltpu.make_async_copy(x_hbm.at[0, :, pl.ds(j * C, C)], xres.at[j], x_sem) for j in range(NC)]
-    for copy in x_copies:
+    x_copies = [pltpu.make_async_copy(x_hbm.at[0, :, pl.ds(j * C, C)], xres.at[j], x_sem.at[j]) for j in range(NC)]
+    g_copies = [pltpu.make_async_copy(g1_hbm, g1_ref, g_sem.at[0]), pltpu.make_async_copy(g2_hbm, g2_ref, g_sem.at[1])]
+    for copy in x_copies + g_copies:
         copy.start()
     for i in range(SLOTS):
         start_attention_tile(0, i)
@@ -167,7 +175,7 @@
     for peer in (partner, cross):
         pl.semaphore_signal(barrier, inc=1, device_id={'tp': peer}, device_id_type=MESH)
     pl.semaphore_wait(barrier, 2)
-    for copy in x_copies:
+    for copy in x_copies + g_copies:
         copy.wait()
 
     def loop(lo, hi, body):
@@ -177,104 +185,114 @@
         norm_and_send(g1_ref, layer)
         forward(0)
 
-        def qkv_chunk(j, first):
+        def qkv_tiles(j, thirds, first):
+            for t in thirds:
+                wait_tile(3 * j + t)
+            block([([(lambda: a_all[j].reshape(SEQ, C), 3 * j + t)], t, not first, None) for t in thirds])
+            for t in thirds:
+                start_up(layer, 3 * j + t)
+
+        def qkv_chunk(j, first, last):
             ag_wait(j, 0)
             ag_wait(j, 2)
-
-            def third(s):
-                i = 3 * j + s
-                wait_tile(i)
-                step(a_all[j], i, s, first)
-                start_up(layer, i)
-
-            third(0)
-
-            @pl.when(j < NC - 1)
-            def _():
+            if last:
+                qkv_tiles(j, (0, 1, 2), first)
+            else:
+                qkv_tiles(j, (0,), first)
                 forward(j + 1)
-
-            loop(1, 3, third)
-
-        qkv_chunk(0, True)
-        loop(1, NC, lambda j: qkv_chunk(j, False))
+                qkv_tiles(j, (1, 2), first)
+
+        qkv_chunk(0, True, False)
+        loop(1, NC - 1, lambda j: qkv_chunk(j, False, False))
+        qkv_chunk(NC - 1, False, True)
         ag_drain()
         attention()
 
-        def out_quarter(q):
-            wait_tile(12 + q)
-            step(att[...], 12 + q, q, True)
-            start_up(layer, 12 + q)
-            rs_a(q)
-
-            @pl.when(q >= 2)
-            def _():
-                rs_b(q - 2)
-
-        loop(0, NC, out_quarter)
-        rs_b(2)
-        rs_b(3)
+        def out_tiles(quarters):
+            for q in quarters:
+                wait_tile(12 + q)
+            block([([(lambda: att[...], 12 + q)], q, False, None) for q in quarters])
+            for q in quarters:
+                rs_a(q)
+            for q in quarters:
+                start_up(layer, 12 + q)
+
+        out_tiles((0, 1))
+        out_tiles((2, 3))
+        loop(0, NC, rs_b)
         loop(0, NC, rs_c)
         rs_drain()
 
         norm_and_send(g2_ref, layer)
         forward(0)
+
+        def gelu_out(part, q, cols):
+            hid[q, :, cols] = jax.nn.gelu(part, approximate=True).astype(jnp.bfloat16)
+
+        def up_tiles(j, quarters, first, last):
+            for q in quarters:
+                wait_tile(NC * j + q)
+            block([([(lambda: a_all[j].reshape(SEQ, C), NC * j + q)], q, not first, gelu_out if last else None)
+                   for q in quarters])
+            for q in quarters:
+                start_down(layer, NC * j + q)
 
         def up_chunk(j, first, last):
             ag_wait(j, 0)
             ag_wait(j, 2)
-
-            def quarter(q):
-                i = NC * j + q
-
-                def finish(part, cols):
-                    hid[q, :, cols] = jax.nn.gelu(part, approximate=True).astype(jnp.bfloat16)
-
-                wait_tile(i)
-                step(a_all[j], i, q, first, finish if last else None)
-                start_down(layer, i)
-
-            quarter(0)
-            if not last:
+            if last:
+                up_tiles(j, (0, 1, 2, 3), first, last)
+            else:
+                up_tiles(j, (0, 1), first, last)
                 forward(j + 1)
-            loop(1, NC, quarter)
+                up_tiles(j, (2, 3), first, last)
 
         up_chunk(0, True, False)
         loop(1, NC - 1, lambda j: up_chunk(j, False, False))
         up_chunk(NC - 1, False, True)
         ag_drain()
 
-        def next_tiles(i):
+        def next_tiles(q, chunks):
             @pl.when(layer < LAYERS - 1)
             def _():
-                for k in range(SLOTS):
-                    @pl.when(i == k)
-                    def _():
-                        start_attention_tile(layer + 1, k)
+                if isinstance(q, int):
+                    for j in chunks:
+                        start_attention_tile(layer + 1, NC * q + j)
+                else:
+                    for k in range(NC - 1):
+                        @pl.when(q == k)
+                        def _():
+                            for j in chunks:
+                                start_attention_tile(layer + 1, NC * k + j)
+
+        def down_tiles(q, chunks, add):
+            for j in chunks:
+                wait_tile(NC * q + j)
+            block([([(functools.partial(lambda j: hid[j], j), NC * q + j) for j in chunks], q, add, None)])
 
         def down_quarter(q):
-            def chunk(j, first):
-                i = NC * q + j
-                wait_tile(i)
-                step(hid[j], i, q, first)
-                next_tiles(i)
-
-            chunk(0, True)
-            chunk(1, False)
+            down_tiles(q, (0, 1, 2, 3), False)
+            rs_a(q)
+            next_tiles(q, (0, 1, 2, 3))
 
             @pl.when(q >= 1)
             def _():
                 rs_b(q - 1)
 
-            loop(2, NC, lambda j: chunk(j, False))
-            rs_a(q)
-
-        loop(0, NC, down_quarter)
-        rs_b(NC - 1)
+        loop(0, NC - 1, down_quarter)
+        last = NC - 1
+        down_tiles(last, (0, 1), False)
+        rs_b(last - 1)
+        next_tiles(last, (0, 1))
+        down_tiles(last, (2, 3), True)
+        rs_a(last)
+        next_tiles(last, (2, 3))
+        rs_b(last)
         loop(0, NC, rs_c)
         rs_drain()
 
     loop(0, LAYERS, layer_body)
-    y_copies = [pltpu.make_async_copy(xres.at[j], y_hbm.at[0, :, pl.ds(j * C, C)], x_sem) for j in range(NC)]
+    y_copies = [pltpu.make_async_copy(xres.at[j], y_hbm.at[0, :, pl.ds(j * C, C)], x_sem.at[j]) for j in range(NC)]
     for copy in y_copies:
         copy.start()
     for copy in y_copies:
@@ -286,12 +304,11 @@
         w_qkv = jnp.transpose(w_qkv, (0, 2, 1, 3))
         w_out = w_out.reshape(LAYERS, HEADS * HD, D)
         hbm = pl.BlockSpec(memory_space=pl.ANY)
-        vmem = pl.BlockSpec(memory_space=pltpu.VMEM)
         weight_bytes = 2 * LAYERS * (3 * C * D + C * D + 2 * D * D)
         return pl.pallas_call(
             stack_kernel,
             out_shape=jax.ShapeDtypeStruct(x_local.shape, jnp.bfloat16),
-            in_specs=[hbm, vmem, hbm, hbm, vmem, hbm, hbm],
+            in_specs=[hbm] * 7,
             out_specs=hbm,
             scratch_shapes=[
                 pltpu.VMEM((SLOTS, C, C), jnp.bfloat16),
@@ -299,13 +316,18 @@
                 pltpu.VMEM((NC, SEQ, C), jnp.bfloat16),
                 pltpu.VMEM((NC, TP, ROWS, C), jnp.float32),
                 pltpu.VMEM((SEQ, C), jnp.bfloat16),
+                pltpu.VMEM((HEADS, SEQ, SEQ), jnp.float32),
+                pltpu.VMEM((HEADS, SEQ, SEQ), jnp.bfloat16),
                 pltpu.VMEM((NC, ROWS, C), jnp.bfloat16),
                 pltpu.VMEM((NC, 2, ROWS, C), jnp.bfloat16),
                 pltpu.VMEM((NC, 2, ROWS, C), jnp.bfloat16),
                 pltpu.VMEM((NC, ROWS, C), jnp.bfloat16),
                 pltpu.VMEM((NC, ROWS, C), jnp.bfloat16),
+                pltpu.VMEM((LAYERS, D), jnp.float32),
+                pltpu.VMEM((LAYERS, D), jnp.float32),
                 pltpu.SemaphoreType.DMA((SLOTS,)),
-                pltpu.SemaphoreType.DMA,
+                pltpu.SemaphoreType.DMA((NC,)),
+                pltpu.SemaphoreType.DMA((2,)),
                 pltpu.SemaphoreType.DMA((3, NC)),
                 pltpu.SemaphoreType.DMA((3, NC)),
                 pltpu.SemaphoreType.DMA((NC,)),

time: 124 us -> 113 us (0.911)
  Pallas kernels: 122 us -> 111 us
    pallas_call x1, Pallas kernels: 122 us -> 111 us  [layer_stack(): pl.pallas_call(stack_kernel, out_shape=jax.ShapeDtypeStruct(x_local.shape...]
where the time goes in v2:
time: 113 us
  Pallas kernels  111 us (98%)
  local copies, waits for them, and re-layouts  1.72 us (2%)
    pallas_call x1, Pallas kernels, layer_stack(): pl.pallas_call(stack_kernel, out_shape=jax.ShapeDtypeStruct(x_local.shape...  111 us

profile of v2, /device:TPU:0, one launch (start us, length us, event | category | flops | bytes accessed | tf_op | source)
XLA Modules:
  0.0 113.0 jit_solution(7116320325625765818)
XLA Ops:
  0.0 111.3 %shard_map.73 = bf16[1,32,5120]{2,1,0:T(8,128)(2,1)} custom-call(bf16[1,32,5120]{2,1,0:T(8,128)(2,1)} %x_hbm.1, f32[2,5120]{1,0:T(2,128)} %g1_hbm.1, bf16[2,10,5120,384]{3,2,1,0:T(8,128)(2,1)} %bitcast.wqkv_hbm, bf16[2,1280,5120]{2,1,0:T(8,128)(2,1)} %bitcast.2, f32[2,5120]{1,0:T(2,128)} %g2_hbm.1, bf16[2,5120,5120]{2,1,0:T(8,128)(2,1)} %wup_hbm.1, ...), custom_call_target="tpu_custom_call" | custom-call | flops 40265318400 | bytes 314572800 | tf_op jit(solution)/shard_map/pallas_call | solution.py:308
  111.3 1.7 %copy.9 = bf16[1,32,5120]{2,1,0:T(8,128)(2,1)} copy(bf16[1,32,5120]{2,1,0:T(8,128)(2,1)} %shard_map.73) | data formatting | bytes 655360

commit v3 on v2

--- a/solution.py
+++ b/solution.py
@@ -25,8 +25,8 @@
 
 
 def stack_kernel(x_hbm, g1_hbm, wqkv_hbm, wout_hbm, g2_hbm, wup_hbm, wdown_hbm, y_hbm,
-                 ring, a_all, hid, acc, att, s_buf, p_buf, xres, p_snd, p_rcv, q_snd, q_rcv, g1_ref, g2_ref,
-                 ring_sem, x_sem, g_sem, ag_s, ag_r, p_s, p_r, q_s, q_r):
+                 ring, x_all, a_buf, stat, q_stat, mean_b, scale_b, hid, acc, att, s_buf, p_buf, p_snd, p_rcv, q_snd, q_rcv, g1_ref, g2_ref,
+                 ring_sem, x_sem, g_sem, ag_s, ag_r, st_s, st_r, p_s, p_r, q_s, q_r):
     me = lax.axis_index('tp')
     partner = me + 1 - 2 * lax.rem(me, 2)
     cross = lax.rem(me + 2, TP)
@@ -85,37 +85,72 @@
                                             device_id={'tp': peer}, device_id_type=MESH)
 
     def ag_copy(j, kind):
-        block, peer = ((me, partner), (me, cross), (cross, partner))[kind]
-        return remote(a_all.at[j, block], a_all.at[j, block], ag_s.at[kind, j], ag_r.at[kind, j], peer)
+        source, peer = ((me, partner), (me, cross), (cross, partner))[kind]
+        return remote(x_all.at[j, source], x_all.at[j, source], ag_s.at[kind, j], ag_r.at[kind, j], peer)
 
     def ag_wait(j, kind):
-        block = (partner, cross, diag)[kind]
-        remote(a_all.at[j, block], a_all.at[j, block], ag_s.at[kind, j], ag_r.at[kind, j], partner).wait_recv()
-
-    def norm_and_send(g_ref, layer):
-        total = jnp.zeros((ROWS, 1), jnp.float32)
-        for j in range(NC):
-            total += jnp.sum(xres[j].astype(jnp.float32), axis=-1, keepdims=True)
-        mean = total / D
-        total = jnp.zeros((ROWS, 1), jnp.float32)
-        for j in range(NC):
-            centered = xres[j].astype(jnp.float32) - mean
-            total += jnp.sum(centered * centered, axis=-1, keepdims=True)
-        scale = lax.rsqrt(total / D + LN_EPS)
-        for j in range(NC):
-            gain = g_ref[pl.ds(layer, 1), pl.ds(j * C, C)]
-            a_all[j, me] = ((xres[j].astype(jnp.float32) - mean) * scale * gain).astype(jnp.bfloat16)
-            ag_copy(j, 1).start()
-            ag_copy(j, 0).start()
+        source = (partner, cross, diag)[kind]
+        remote(x_all.at[j, source], x_all.at[j, source], ag_s.at[kind, j], ag_r.at[kind, j], partner).wait_recv()
+
+    def ag_send(j):
+        ag_copy(j, 1).start()
+        ag_copy(j, 0).start()
 
     def forward(j):
         ag_wait(j, 1)
         ag_copy(j, 2).start()
+
+    def stat_copy(k):
+        return remote(stat.at[me], stat.at[me], st_s.at[k], st_r.at[k], (partner, cross, diag)[k])
+
+    def quarter_stats(j):
+        x = x_all[j, me].astype(jnp.float32)
+        mean = jnp.sum(x, axis=-1, keepdims=True) / C
+        centered = x - mean
+        q_stat[j, 0] = jnp.broadcast_to(mean, (ROWS, HD))
+        q_stat[j, 1] = jnp.broadcast_to(jnp.sum(centered * centered, axis=-1, keepdims=True), (ROWS, HD))
+
+    def stats_send():
+        mean = (q_stat[0, 0] + q_stat[1, 0] + q_stat[2, 0] + q_stat[3, 0]) / NC
+        square = jnp.zeros((ROWS, HD), jnp.float32)
+        for j in range(NC):
+            shift = q_stat[j, 0] - mean
+            square += q_stat[j, 1] + C * (shift * shift)
+        scale = lax.rsqrt(square / D + LN_EPS)
+        lanes = lax.broadcasted_iota(jnp.int32, (8, HD), 1)
+        packed = jnp.zeros((8, HD), jnp.float32)
+        for i in range(ROWS // 8):
+            packed = jnp.where(lanes == i, mean[8 * i:8 * i + 8], packed)
+            packed = jnp.where(lanes == 4 + i, scale[8 * i:8 * i + 8], packed)
+        stat[me] = packed
+        for k in (1, 2, 0):
+            stat_copy(k).start()
+
+    def stats_wait():
+        for k, source in enumerate((partner, cross, diag)):
+            remote(stat.at[source], stat.at[source], st_s.at[k], st_r.at[k], partner).wait_recv()
+        for source in range(TP):
+            packed = stat[source]
+            for i in range(ROWS // 8):
+                rows = pl.ds(source * ROWS + 8 * i, 8)
+                mean_b[rows] = jnp.broadcast_to(packed[:, i:i + 1], (8, HD))
+                scale_b[rows] = jnp.broadcast_to(packed[:, 4 + i:5 + i], (8, HD))
 
     def ag_drain():
         for j in range(NC):
             for kind in range(3):
                 ag_copy(j, kind).wait_send()
+        for k in range(3):
+            stat_copy(k).wait_send()
+
+    def normalize(j, g_ref, layer):
+        mean, scale = mean_b[...], scale_b[...]
+        for k in range(C // HD):
+            cols = pl.ds(k * HD, HD)
+            gains = g_ref[:, pl.ds(pl.multiple_of(j * C + k * HD, HD), HD)]
+            gain = jnp.where(layer == 0, gains[0:1], gains[1:2])
+            x = x_all[j, :, :, cols].reshape(SEQ, HD).astype(jnp.float32)
+            a_buf[:, cols] = ((x - mean) * scale * gain).astype(jnp.bfloat16)
 
     def rs_p(q):
         return remote(p_snd.at[q], p_rcv.at[q], p_s.at[q], p_r.at[q], partner)
@@ -136,7 +171,8 @@
     def rs_c(q):
         rs_q(q).wait_recv()
         total = acc[q, me] + p_rcv[q, 0].astype(jnp.float32) + q_rcv[q].astype(jnp.float32)
-        xres[q] = (xres[q].astype(jnp.float32) + total).astype(jnp.bfloat16)
+        x_all[q, me] = (x_all[q, me].astype(jnp.float32) + total).astype(jnp.bfloat16)
+        quarter_stats(q)
 
     def rs_drain():
         for q in range(NC):
@@ -165,47 +201,56 @@
                                   preferred_element_type=jnp.float32)
             att[:, pl.ds(head * HD, HD)] = out.astype(jnp.bfloat16)
 
-    x_copies = [pltpu.make_async_copy(x_hbm.at[0, :, pl.ds(j * C, C)], xres.at[j], x_sem.at[j]) for j in range(NC)]
+    x_copies = [pltpu.make_async_copy(x_hbm.at[0, :, pl.ds(j * C, C)], x_all.at[j, me], x_sem.at[j]) for j in range(NC)]
     g_copies = [pltpu.make_async_copy(g1_hbm, g1_ref, g_sem.at[0]), pltpu.make_async_copy(g2_hbm, g2_ref, g_sem.at[1])]
     for copy in x_copies + g_copies:
         copy.start()
     for i in range(SLOTS):
         start_attention_tile(0, i)
     barrier = pltpu.get_barrier_semaphore()
-    for peer in (partner, cross):
+    for peer in (partner, cross, diag):
         pl.semaphore_signal(barrier, inc=1, device_id={'tp': peer}, device_id_type=MESH)
-    pl.semaphore_wait(barrier, 2)
+    pl.semaphore_wait(barrier, 3)
     for copy in x_copies + g_copies:
         copy.wait()
 
     def loop(lo, hi, body):
         lax.fori_loop(lo, hi, lambda i, carry: (body(i), carry)[1], 0)
 
-    def layer_body(layer):
-        norm_and_send(g1_ref, layer)
-        forward(0)
-
-        def qkv_tiles(j, thirds, first):
-            for t in thirds:
-                wait_tile(3 * j + t)
-            block([([(lambda: a_all[j].reshape(SEQ, C), 3 * j + t)], t, not first, None) for t in thirds])
-            for t in thirds:
-                start_up(layer, 3 * j + t)
-
-        def qkv_chunk(j, first, last):
+    def chunks(chunk):
+        stats_wait()
+
+        def one(j, first, last):
             ag_wait(j, 0)
             ag_wait(j, 2)
-            if last:
-                qkv_tiles(j, (0, 1, 2), first)
-            else:
-                qkv_tiles(j, (0,), first)
-                forward(j + 1)
-                qkv_tiles(j, (1, 2), first)
-
-        qkv_chunk(0, True, False)
-        loop(1, NC - 1, lambda j: qkv_chunk(j, False, False))
-        qkv_chunk(NC - 1, False, True)
+            chunk(j, first, last)
+
+        one(0, True, False)
+        forward(2)
+
+        def middle(j):
+            one(j, False, False)
+
+            @pl.when(j == 1)
+            def _():
+                forward(3)
+
+        loop(1, NC - 1, middle)
+        one(NC - 1, False, True)
         ag_drain()
+
+    def layer_body(layer):
+        more = layer < LAYERS - 1
+
+        def qkv_chunk(j, first, last):
+            for t in range(3):
+                wait_tile(3 * j + t)
+            normalize(j, g1_ref, layer)
+            block([([(lambda: a_buf[...], 3 * j + t)], t, not first, None) for t in range(3)])
+            for t in range(3):
+                start_up(layer, 3 * j + t)
+
+        chunks(qkv_chunk)
         attention()
 
         def out_tiles(quarters):
@@ -217,82 +262,93 @@
             for q in quarters:
                 start_up(layer, 12 + q)
 
-        out_tiles((0, 1))
-        out_tiles((2, 3))
-        loop(0, NC, rs_b)
-        loop(0, NC, rs_c)
+        out_tiles((0,))
+        out_tiles((1, 2))
+        rs_b(0)
+        out_tiles((3,))
+        loop(1, NC, rs_b)
+        for q in range(NC):
+            rs_c(q)
+            if q < 2:
+                ag_send(q)
+        stats_send()
+        ag_send(2)
+        ag_send(3)
+        forward(0)
+        forward(1)
         rs_drain()
-
-        norm_and_send(g2_ref, layer)
-        forward(0)
 
         def gelu_out(part, q, cols):
             hid[q, :, cols] = jax.nn.gelu(part, approximate=True).astype(jnp.bfloat16)
 
-        def up_tiles(j, quarters, first, last):
-            for q in quarters:
+        def up_chunk(j, first, last):
+            for q in range(NC):
                 wait_tile(NC * j + q)
-            block([([(lambda: a_all[j].reshape(SEQ, C), NC * j + q)], q, not first, gelu_out if last else None)
-                   for q in quarters])
-            for q in quarters:
+            normalize(j, g2_ref, layer)
+            block([([(lambda: a_buf[...], NC * j + q)], q, not first, gelu_out if last else None) for q in range(NC)])
+            for q in range(NC):
                 start_down(layer, NC * j + q)
 
-        def up_chunk(j, first, last):
-            ag_wait(j, 0)
-            ag_wait(j, 2)
-            if last:
-                up_tiles(j, (0, 1, 2, 3), first, last)
-            else:
-                up_tiles(j, (0, 1), first, last)
-                forward(j + 1)
-                up_tiles(j, (2, 3), first, last)
-
-        up_chunk(0, True, False)
-        loop(1, NC - 1, lambda j: up_chunk(j, False, False))
-        up_chunk(NC - 1, False, True)
-        ag_drain()
-
-        def next_tiles(q, chunks):
-            @pl.when(layer < LAYERS - 1)
-            def _():
-                if isinstance(q, int):
-                    for j in chunks:
-                        start_attention_tile(layer + 1, NC * q + j)
-                else:
-                    for k in range(NC - 1):
-                        @pl.when(q == k)
-                        def _():
-                            for j in chunks:
-                                start_attention_tile(layer + 1, NC * k + j)
-
-        def down_tiles(q, chunks, add):
-            for j in chunks:
+        chunks(up_chunk)
+
+        def down_tiles(q, chunk_ids, add):
+            for j in chunk_ids:
                 wait_tile(NC * q + j)
-            block([([(functools.partial(lambda j: hid[j], j), NC * q + j) for j in chunks], q, add, None)])
+            block([([(functools.partial(lambda j: hid[j], j), NC * q + j) for j in chunk_ids], q, add, None)])
+
+            for k in range(NC):
+                @pl.when(jnp.logical_and(more, q == k))
+                def _():
+                    for j in chunk_ids:
+                        start_attention_tile(layer + 1, NC * k + j)
 
         def down_quarter(q):
-            down_tiles(q, (0, 1, 2, 3), False)
-            rs_a(q)
-            next_tiles(q, (0, 1, 2, 3))
+            down_tiles(q, (0, 1), False)
 
             @pl.when(q >= 1)
             def _():
                 rs_b(q - 1)
 
-        loop(0, NC - 1, down_quarter)
-        last = NC - 1
-        down_tiles(last, (0, 1), False)
-        rs_b(last - 1)
-        next_tiles(last, (0, 1))
-        down_tiles(last, (2, 3), True)
-        rs_a(last)
-        next_tiles(last, (2, 3))
-        rs_b(last)
-        loop(0, NC, rs_c)
+            @pl.when(q >= 2)
+            def _():
+                rs_c(q - 2)
+
+                @pl.when(more)
+                def _():
+                    ag_send(q - 2)
+
+            down_tiles(q, (2, 3), True)
+            rs_a(q)
+
+        loop(0, NC, down_quarter)
+        rs_b(3)
+        rs_c(2)
+
+        @pl.when(more)
+        def _():
+            ag_send(2)
+            forward(0)
+            forward(1)
+
+        rs_c(3)
+
+        @pl.when(more)
+        def _():
+            stats_send()
+            ag_send(3)
+
         rs_drain()
 
+    ag_send(0)
+    for j in range(NC):
+        quarter_stats(j)
+    stats_send()
+    for j in range(1, NC):
+        ag_send(j)
+    forward(0)
+    forward(1)
     loop(0, LAYERS, layer_body)
-    y_copies = [pltpu.make_async_copy(xres.at[j], y_hbm.at[0, :, pl.ds(j * C, C)], x_sem.at[j]) for j in range(NC)]
+    y_copies = [pltpu.make_async_copy(x_all.at[j, me], y_hbm.at[0, :, pl.ds(j * C, C)], x_sem.at[j]) for j in range(NC)]
     for copy in y_copies:
         copy.start()
     for copy in y_copies:
@@ -313,12 +369,16 @@
             scratch_shapes=[
                 pltpu.VMEM((SLOTS, C, C), jnp.bfloat16),
                 pltpu.VMEM((NC, TP, ROWS, C), jnp.bfloat16),
+                pltpu.VMEM((SEQ, C), jnp.bfloat16),
+                pltpu.VMEM((TP, 8, HD), jnp.float32),
+                pltpu.VMEM((NC, 2, ROWS, HD), jnp.float32),
+                pltpu.VMEM((SEQ, HD), jnp.float32),
+                pltpu.VMEM((SEQ, HD), jnp.float32),
                 pltpu.VMEM((NC, SEQ, C), jnp.bfloat16),
                 pltpu.VMEM((NC, TP, ROWS, C), jnp.float32),
                 pltpu.VMEM((SEQ, C), jnp.bfloat16),
                 pltpu.VMEM((HEADS, SEQ, SEQ), jnp.float32),
                 pltpu.VMEM((HEADS, SEQ, SEQ), jnp.bfloat16),
-                pltpu.VMEM((NC, ROWS, C), jnp.bfloat16),
                 pltpu.VMEM((NC, 2, ROWS, C), jnp.bfloat16),
                 pltpu.VMEM((NC, 2, ROWS, C), jnp.bfloat16),
                 pltpu.VMEM((NC, ROWS, C), jnp.bfloat16),
@@ -330,6 +390,8 @@
                 pltpu.SemaphoreType.DMA((2,)),
                 pltpu.SemaphoreType.DMA((3, NC)),
                 pltpu.SemaphoreType.DMA((3, NC)),
+                pltpu.SemaphoreType.DMA((3,)),
+                pltpu.SemaphoreType.DMA((3,)),
                 pltpu.SemaphoreType.DMA((NC,)),
                 pltpu.SemaphoreType.DMA((NC,)),
                 pltpu.SemaphoreType.DMA((NC,)),

time: 113 us -> 110 us (0.973)
  Pallas kernels: 111 us -> 108 us
    pallas_call x1, Pallas kernels: 111 us -> 108 us  [layer_stack(): pl.pallas_call(stack_kernel, out_shape=jax.ShapeDtypeStruct(x_local.shape...]
where the time goes in v3:
time: 110 us
  Pallas kernels  108 us (98%)
  local copies, waits for them, and re-layouts  1.72 us (2%)
    pallas_call x1, Pallas kernels, layer_stack(): pl.pallas_call(stack_kernel, out_shape=jax.ShapeDtypeStruct(x_local.shape...  108 us

profile of v3, /device:TPU:0, one launch (start us, length us, event | category | flops | bytes accessed | tf_op | source)
XLA Modules:
  0.0 110.1 jit_solution(6993114086128740344)
XLA Ops:
  0.0 108.4 %shard_map.73 = bf16[1,32,5120]{2,1,0:T(8,128)(2,1)} custom-call(bf16[1,32,5120]{2,1,0:T(8,128)(2,1)} %x_hbm.1, f32[2,5120]{1,0:T(2,128)} %g1_hbm.1, bf16[2,10,5120,384]{3,2,1,0:T(8,128)(2,1)} %bitcast.wqkv_hbm, bf16[2,1280,5120]{2,1,0:T(8,128)(2,1)} %bitcast.2, f32[2,5120]{1,0:T(2,128)} %g2_hbm.1, bf16[2,5120,5120]{2,1,0:T(8,128)(2,1)} %wup_hbm.1, ...), custom_call_target="tpu_custom_call" | custom-call | flops 40265318400 | bytes 314572800 | tf_op jit(solution)/shard_map/pallas_call | solution.py:364
  108.4 1.7 %copy.9 = bf16[1,32,5120]{2,1,0:T(8,128)(2,1)} copy(bf16[1,32,5120]{2,1,0:T(8,128)(2,1)} %shard_map.73) | data formatting | bytes 655360
